TPU v7x, 32 devices: a whole 2x2x4 slice. The times are simulated.
32 devices in a mesh: grp: 4 (over y, x), mem: 8 (over z, core).
Axes of the slice: x: 2, y: 2, z: 4, core: 2. Of those that a mesh axis runs over, the one named last changes fastest.
Arguments:
- weight: bfloat16 [2, 16384, 16384], P(None, None, ('grp', 'mem')), may hold values from -0.046875 to 0.046875
- activation: bfloat16 [2, 16384, 512], P(None, ('grp', 'mem')), may hold values from -6 to 6
- points: int32 [4], replicated, may hold values from 0 to 3, each once
Outputs:
- share: float32 [4, 16384, 512], P('grp', 'mem')
Inputs may be any that keep to these rules, and one draw needn't show every extreme that they name: A permutation of 0 to 3; group g evaluates at points[g] + 1.
All inputs are finite; a program needn't handle non-finite values.
Results may differ from a plain program's by a relative error of at most 0.0042.
Values may be sent and summed in bfloat16 or wider, within the bound.
A program may use at most 320 MiB of HBM per device.

v0:
```python
import jax
import jax.numpy as jnp
from jax import lax
from jax.sharding import PartitionSpec as P


def code_stack(raw_blocks, factors):
    total = factors[:, 0, None, None] * raw_blocks[0].astype(jnp.float32)[None]
    for block in range(1, raw_blocks.shape[0]):
        total = total + factors[:, block, None, None] * raw_blocks[block].astype(jnp.float32)[None]
    return total.astype(jnp.bfloat16)


def per_device(weight, activation, points):
    groups = lax.axis_size("grp")
    blocks = weight.shape[0]
    splits = activation.shape[0]
    anchors = (points + 1).astype(jnp.float32) / groups
    factors = anchors[:, None] ** jnp.arange(blocks, dtype=jnp.float32)[None, :]
    lifts_all = anchors[:, None] ** (jnp.arange(splits, dtype=jnp.float32) * blocks)[None, :]
    slab = lax.all_to_all(weight, "mem", split_axis=1, concat_axis=2, tiled=True)
    block_input = lax.all_gather(activation, "mem", axis=1, tiled=True)
    coded_weight = code_stack(slab, factors)
    coded_input = code_stack(block_input, lifts_all)
    return lax.psum_scatter(
        jnp.einsum("grk,gkc->grc", coded_weight, coded_input, preferred_element_type=jnp.float32),
        "grp",
        scatter_dimension=0,
        tiled=True,
    )


def solution(mesh):
    placed = (P(None, None, ("grp", "mem")), P(None, ("grp", "mem"), None), P())
    return jax.shard_map(
        per_device, mesh=mesh, in_specs=placed, out_specs=P("grp", "mem", None), check_vma=False
    )
```

profile of v0, /device:TPU:0, one launch (start us, length us, event | category | flops | bytes accessed | tf_op | source)
XLA Modules:
  0.0 1254.2 jit_solution(2382327408538441488)
XLA Ops:
  6.5 60.1 %copy.10 = bf16[2,16384,512]{2,0,1:T(2,128)(2,1)} copy(bf16[2,16384,512]{2,1,0:T(8,128)(2,1)} %param.3) | data formatting | bytes 67108864 | tf_op args[0]
  66.6 0.0 copy-start
  66.6 7.2 all-to-all-start
  73.9 0.0 all-gather.2.cloned.1.call-start
  73.9 0.7 all-gather.2.cloned.1.call-update
  74.6 0.0 reduce-scatter.4.cloned.1.call-start
  74.7 0.0 copy-done
  74.7 0.1 broadcast_power_fusion
  74.8 154.4 %all-gather.2.cloned.1.call-done = bf16[2,4096,512]{2,1,0:T(8,128)(2,1)} async-done(((bf16[2,512,512]{2,1,0:T(8,128)(2,1)}), bf16[2,4096,512]{2,1,0:T(8,128)(2,1)}) %all-gather.2.cloned.1.call-update) | async-done | bytes 8388624 | tf_op jit(solution)/shard_map/all_gather | solution.py:22
  229.1 11.7 fusion.10
  240.9 15.1 %add_convert_fusion.10 = bf16[4,4096,512]{2,1,0:T(8,128)(2,1)} fusion(f32[4096,512]{1,0:T(8,128)} %get-tuple-element.8, f32[4]{0:T(128)S(1)} %get-tuple-element.10, f32[4096,512]{1,0:T(8,128)} %get-tuple-element.7, f32[4]{0:T(128)S(1)} %get-tuple-element.9), kind=kLoop, calls=%fused_computation.6.clone.clone.2 | loop fusion | flops 33554432 | bytes 33554464 | tf_op jit(solution)/shard_map/grk,gkc->grc/dot_general | solution.py:26
  256.0 609.3 %all-to-all-done = bf16[2,16384,512]{2,0,1:T(2,128)(2,1)} async-done(((bf16[2,16384,512]{2,0,1:T(2,128)(2,1)}), bf16[2,16384,512]{2,0,1:T(2,128)(2,1)}, u32[]{:S(2)}, u32[]{:S(2)}) %all-to-all-start) | async-done | bytes 33554464 | tf_op jit(solution)/shard_map/all_to_all | solution.py:21
  865.3 22.7 %copy.11 = bf16[2,16384,512]{2,1,0:T(8,128)(2,1)} copy(bf16[2,16384,512]{2,0,1:T(2,128)(2,1)} %all-to-all-done) | data formatting | bytes 67108864 | tf_op jit(solution)/shard_map/all_to_all | solution.py:21
  888.0 34.1 %slice_convert_fusion.1 = (f32[1,2048,8,512]{3,1,2,0:T(8,128)}, f32[1,2048,8,512]{3,1,2,0:T(8,128)}) fusion(bf16[2,2048,8,512]{3,1,2,0:T(8,128)(2,1)} %bitcast.25), kind=kLoop, calls=%fused_computation.8 | loop fusion | flops 16777216 | bytes 100663296 | tf_op jit(solution)/shard_map/convert_element_type | solution.py:8
  922.1 31.8 %copy.14 = f32[1,2048,8,512]{1,3,2,0:T(8,128)} copy(f32[1,2048,8,512]{3,1,2,0:T(8,128)} %get-tuple-element.6) | data formatting | bytes 67108864 | tf_op jit(solution)/shard_map/convert_element_type | solution.py:10
  953.9 31.1 %copy.15 = f32[2048,4096]{1,0:T(8,128)} copy(f32[2048,4096]{0,1:T(8,128)} %bitcast.26) | data formatting | bytes 67108864 | tf_op jit(solution)/shard_map/convert_element_type | solution.py:10
  985.0 31.8 %copy.12 = f32[1,2048,8,512]{1,3,2,0:T(8,128)} copy(f32[1,2048,8,512]{3,1,2,0:T(8,128)} %get-tuple-element.5) | data formatting | bytes 67108864 | tf_op jit(solution)/shard_map/convert_element_type | solution.py:8
  1016.8 31.1 %copy.13 = f32[2048,4096]{1,0:T(8,128)} copy(f32[2048,4096]{0,1:T(8,128)} %bitcast.27) | data formatting | bytes 67108864 | tf_op jit(solution)/shard_map/convert_element_type | solution.py:8
  1047.9 46.0 %fusion = f32[4,2048,512]{2,1,0:T(8,128)} fusion(f32[2048,4096]{1,0:T(8,128)} %copy.15, f32[4]{0:T(128)S(1)} %get-tuple-element.15, f32[2048,4096]{1,0:T(8,128)} %copy.13, f32[4]{0:T(128)S(1)} %get-tuple-element.16, bf16[4,4096,512]{2,1,0:T(8,128)(2,1)} %add_convert_fusion.10), kind=kOutput, calls=%fused_computation.1 | convolution fusion | flops 34493956096 | bytes 100663328 | tf_op jit(solution)/shard_map/grk,gkc->grc/dot_general | solution.py:26
  1093.9 0.0 reduce-scatter.4.cloned.1.call-update
  1094.0 153.4 %reduce-scatter.4.cloned.1.call-done = f32[1,2048,512]{2,1,0:T(8,128)} async-done(((f32[4,2048,512]{2,1,0:T(8,128)}), f32[1,2048,512]{2,1,0:T(8,128)}) %reduce-scatter.4.cloned.1.call-update) | async-done | bytes 4194320
  (3 shorter events, 0.0 us)
Async XLA Ops:
  66.6 8.0 copy-start
  66.6 798.7 %all-to-all-start = ((bf16[2,16384,512]{2,0,1:T(2,128)(2,1)}), bf16[2,16384,512]{2,0,1:T(2,128)(2,1)}, u32[]{:S(2)}, u32[]{:S(2)}) async-start(bf16[2,16384,512]{2,0,1:T(2,128)(2,1)} %copy.10), calls=%async_computation | async-start | bytes 67108864 | tf_op jit(solution)/shard_map/all_to_all | solution.py:21
  73.9 155.3 %all-gather.2.cloned.1.call-start = ((), (), s32[]{:S(2)}) async-start(), calls=%async_computation.2 | async-start | bytes 9437184 | tf_op jit(solution)/shard_map/all_gather | solution.py:22
  74.6 1172.8 %reduce-scatter.4.cloned.1.call-start = ((), (), s32[]{:S(2)}) async-start(), calls=%async_computation.3 | async-start | bytes 20971520
Sparse Core Ops, SparseCore 0:
  76.3 152.8 all-gather.1
  1094.1 153.2 reduce-scatter.3
where the time goes:
time: 1260 us; the launch traced here: 1250 us
  waiting for transfers between devices  918 us (73%)
  local copies, waits for them, and re-layouts  209 us (17%)
  other arithmetic  60.9 us (5%)
  matrix products  46 us (4%)
  between operations  13.5 us (1%)
    all_to_all x1, waiting for transfers between devices, per_device(): lax.all_to_all(weight, 'mem', split_axis=1, concat_axis=2, tiled=True)  609 us
    all_gather x1, waiting for transfers between devices, per_device(): block_input = lax.all_gather(activation, 'mem', axis=1, tiled=True)  154 us
    unnamed x3, waiting for transfers between devices  154 us
    convert_element_type x2, local copies, waits for them, and re-layouts, code_stack(): raw_blocks[block].astype(jnp.float32)[None]  62.9 us
    convert_element_type x2, local copies, waits for them, and re-layouts, code_stack(): total = factors[:, 0, None, None] * raw_blocks[0].astype(jnp.float32)[None]  62.9 us
    unnamed x3, local copies, waits for them, and re-layouts  60.1 us
    dot_general x1, matrix products, per_device(): jnp.einsum('grk,gkc->grc', coded_weight, coded_input, preferred_element_t...  46 us
    convert_element_type x1, other arithmetic, code_stack(): total = factors[:, 0, None, None] * raw_blocks[0].astype(jnp.float32)[None]  34.1 us
  transfers between devices with their start and end apart: 3, of which 3 were waited for; matrix products, arithmetic and copies ran while one was open for 2% of the time, Pallas kernels for 0%

commit v1 on v0

--- a/solution.py
+++ b/solution.py
@@ -19,7 +19,12 @@
     factors = anchors[:, None] ** jnp.arange(blocks, dtype=jnp.float32)[None, :]
     lifts_all = anchors[:, None] ** (jnp.arange(splits, dtype=jnp.float32) * blocks)[None, :]
     slab = lax.all_to_all(weight, "mem", split_axis=1, concat_axis=2, tiled=True)
-    block_input = lax.all_gather(activation, "mem", axis=1, tiled=True)
+    ring = [activation]
+    for hop in range(7):
+        ring.append(lax.ppermute(ring[-1], "mem", [(dev, (dev + 1) % 8) for dev in range(8)]))
+    block_input = jnp.roll(
+        jnp.concatenate(ring[::-1], axis=1), (lax.axis_index("mem") + 1) * ring[0].shape[1], axis=1
+    )
     coded_weight = code_stack(slab, factors)
     coded_input = code_stack(block_input, lifts_all)
     return lax.psum_scatter(

time: 1260 us -> 1340 us (1.063)
  starting transfers between devices: 7.3 us -> 195 us
  waiting for transfers between devices: 918 us -> 785 us
  local copies, waits for them, and re-layouts: 209 us -> 237 us
    ppermute x0 -> x7, waiting for transfers between devices: none -> 610 us  [per_device(): lax.ppermute(ring[-1], 'mem', [(dev, (dev + 1) % 8) for dev in range(8)])]
    all_to_all x1, waiting for transfers between devices: 609 us -> 0.01 us  [per_device(): lax.all_to_all(weight, 'mem', split_axis=1, concat_axis=2, tiled=True)]
    ppermute x0 -> x7, starting transfers between devices: none -> 188 us  [per_device(): lax.ppermute(ring[-1], 'mem', [(dev, (dev + 1) % 8) for dev in range(8)])]
    all_gather x1 -> x0, waiting for transfers between devices: 154 us -> none  [per_device(): block_input = lax.all_gather(activation, 'mem', axis=1, tiled=True)]
    unnamed x3 -> x32, local copies, waits for them, and re-layouts: 60.1 us -> 87.2 us
    unnamed x3 -> x2, waiting for transfers between devices: 154 us -> 175 us
  transfers between devices with their start and end apart: 3 -> 9, of which waited for: 3 -> 8; matrix products, arithmetic and copies ran while one was open for 2% -> 4% of each run, Pallas kernels for 0% -> 0%
where the time goes in v1:
time: 1340 us
  waiting for transfers between devices  785 us (59%)
  local copies, waits for them, and re-layouts  237 us (18%)
  starting transfers between devices  195 us (15%)
  other arithmetic  60.9 us (5%)
  matrix products  46.1 us (3%)
  between operations  13.5 us (1%)
    ppermute x7, waiting for transfers between devices, per_device(): lax.ppermute(ring[-1], 'mem', [(dev, (dev + 1) % 8) for dev in range(8)])  610 us
    ppermute x7, starting transfers between devices, per_device(): lax.ppermute(ring[-1], 'mem', [(dev, (dev + 1) % 8) for dev in range(8)])  188 us
    unnamed x2, waiting for transfers between devices  175 us
    unnamed x32, local copies, waits for them, and re-layouts  87.2 us
    convert_element_type x2, local copies, waits for them, and re-layouts, code_stack(): raw_blocks[block].astype(jnp.float32)[None]  63 us
    convert_element_type x2, local copies, waits for them, and re-layouts, code_stack(): total = factors[:, 0, None, None] * raw_blocks[0].astype(jnp.float32)[None]  62.9 us
    dot_general x1, matrix products, per_device(): jnp.einsum('grk,gkc->grc', coded_weight, coded_input, preferred_element_t...  46.1 us
    convert_element_type x1, other arithmetic, code_stack(): total = factors[:, 0, None, None] * raw_blocks[0].astype(jnp.float32)[None]  34.1 us
  transfers between devices with their start and end apart: 9, of which 8 were waited for; matrix products, arithmetic and copies ran while one was open for 4% of the time, Pallas kernels for 0%

profile of v1, /device:TPU:0, one launch (start us, length us, event | category | flops | bytes accessed | tf_op | source)
XLA Modules:
  0.0 1338.0 jit_solution(12676553135009281391)
XLA Ops:
  6.5 60.1 %copy.10 = bf16[2,16384,512]{2,0,1:T(2,128)(2,1)} copy(bf16[2,16384,512]{2,1,0:T(8,128)(2,1)} %param.3) | data formatting | bytes 67108864 | tf_op args[0]
  66.6 7.2 all-to-all-start
  74.5 555.9 %collective-permute-done = bf16[2,512,512]{2,1,0:T(8,128)(2,1)S(1)} collective-permute-done((bf16[2,512,512]{2,1,0:T(8,128)(2,1)S(1)}, bf16[2,512,512]{2,1,0:T(8,128)(2,1)S(1)}, u32[]{:S(2)}, u32[]{:S(2)}) %collective-permute-start) | collective-permute-done | bytes 1048608 | tf_op jit(solution)/shard_map/ppermute | solution.py:24
  630.4 16.1 %collective-permute-done.1 = bf16[2,512,512]{2,1,0:T(8,128)(2,1)S(1)} collective-permute-done((bf16[2,512,512]{2,1,0:T(8,128)(2,1)S(1)}, bf16[2,512,512]{2,1,0:T(8,128)(2,1)S(1)}, u32[]{:S(2)}, u32[]{:S(2)}) %collective-permute-start.1) | collective-permute-done | bytes 1048608 | tf_op jit(solution)/shard_map/ppermute | solution.py:24
  646.5 16.1 %collective-permute-done.2 = bf16[2,512,512]{2,1,0:T(8,128)(2,1)S(1)} collective-permute-done((bf16[2,512,512]{2,1,0:T(8,128)(2,1)S(1)}, bf16[2,512,512]{2,1,0:T(8,128)(2,1)S(1)}, u32[]{:S(2)}, u32[]{:S(2)}) %collective-permute-start.2) | collective-permute-done | bytes 1048608 | tf_op jit(solution)/shard_map/ppermute | solution.py:24
  663.6 158.3 %collective-permute-start.3 = (bf16[2,512,512]{2,1,0:T(8,128)(2,1)S(1)}, bf16[2,512,512]{2,1,0:T(8,128)(2,1)S(1)}, u32[]{:S(2)}, u32[]{:S(2)}) collective-permute-start(bf16[2,512,512]{2,1,0:T(8,128)(2,1)S(1)} %collective-permute-done.2), channel_id=1, source_target_pairs={{0,1},{1,2},{2,3},{3,4},{4,5},{5,6},{6,7},{7,0},{8,9},{9,10},{10,1... | collective-permute-start | bytes 3145736 | tf_op jit(solution)/shard_map/ppermute | solution.py:24
  825.2 11.9 collective-permute-start.4
  837.1 4.5 collective-permute-done.4
  842.6 9.7 collective-permute-start.5
  852.3 6.5 collective-permute-done.5
  858.8 7.7 collective-permute-start.6
  866.7 8.6 collective-permute-done.6
  875.2 2.3 constant_dynamic-update-slice_fusion.15
  889.7 2.3 constant_dynamic-update-slice_fusion.7
  900.5 11.7 fusion.10
  912.2 15.2 %add_convert_fusion.10 = bf16[4,4096,512]{2,1,0:T(8,128)(2,1)} fusion(f32[4096,512]{1,0:T(8,128)} %get-tuple-element.8, f32[4]{0:T(128)S(1)} %get-tuple-element.10, f32[4096,512]{1,0:T(8,128)} %get-tuple-element.7, f32[4]{0:T(128)S(1)} %get-tuple-element.9), kind=kLoop, calls=%fused_computation.6.clone.clone.2 | loop fusion | flops 33554432 | bytes 33554464 | tf_op jit(solution)/shard_map/grk,gkc->grc/dot_general | solution.py:31
  927.4 22.8 %copy.11 = bf16[2,16384,512]{2,1,0:T(8,128)(2,1)} copy(bf16[2,16384,512]{2,0,1:T(2,128)(2,1)} %all-to-all-done) | data formatting | bytes 67108864 | tf_op jit(solution)/shard_map/all_to_all | solution.py:21
  950.2 34.1 %slice_convert_fusion.1 = (f32[1,2048,8,512]{3,1,2,0:T(8,128)}, f32[1,2048,8,512]{3,1,2,0:T(8,128)}) fusion(bf16[2,2048,8,512]{3,1,2,0:T(8,128)(2,1)} %bitcast.25), kind=kLoop, calls=%fused_computation.8 | loop fusion | flops 16777216 | bytes 100663296 | tf_op jit(solution)/shard_map/convert_element_type | solution.py:8
  984.2 31.8 %copy.14 = f32[1,2048,8,512]{1,3,2,0:T(8,128)} copy(f32[1,2048,8,512]{3,1,2,0:T(8,128)} %get-tuple-element.6) | data formatting | bytes 67108864 | tf_op jit(solution)/shard_map/convert_element_type | solution.py:10
  1016.1 31.1 %copy.15 = f32[2048,4096]{1,0:T(8,128)} copy(f32[2048,4096]{0,1:T(8,128)} %bitcast.26) | data formatting | bytes 67108864 | tf_op jit(solution)/shard_map/convert_element_type | solution.py:10
  1047.2 31.8 %copy.12 = f32[1,2048,8,512]{1,3,2,0:T(8,128)} copy(f32[1,2048,8,512]{3,1,2,0:T(8,128)} %get-tuple-element.5) | data formatting | bytes 67108864 | tf_op jit(solution)/shard_map/convert_element_type | solution.py:8
  1079.0 31.1 %copy.13 = f32[2048,4096]{1,0:T(8,128)} copy(f32[2048,4096]{0,1:T(8,128)} %bitcast.27) | data formatting | bytes 67108864 | tf_op jit(solution)/shard_map/convert_element_type | solution.py:8
  1110.1 46.1 %fusion = f32[4,2048,512]{2,1,0:T(8,128)} fusion(f32[2048,4096]{1,0:T(8,128)} %copy.15, f32[4]{0:T(128)S(1)} %get-tuple-element.15, f32[2048,4096]{1,0:T(8,128)} %copy.13, f32[4]{0:T(128)S(1)} %get-tuple-element.16, bf16[4,4096,512]{2,1,0:T(8,128)(2,1)} %add_convert_fusion.10), kind=kOutput, calls=%fused_computation.1 | convolution fusion | flops 34493956096 | bytes 100663328 | tf_op jit(solution)/shard_map/grk,gkc->grc/dot_general | solution.py:31
  1156.2 175.0 %reduce-scatter.4.cloned.1.call-done = f32[1,2048,512]{2,1,0:T(8,128)} async-done(((f32[4,2048,512]{2,1,0:T(8,128)}), f32[1,2048,512]{2,1,0:T(8,128)}) %reduce-scatter.4.cloned.1.call-update) | async-done | bytes 4194320
  (41 shorter events, 26.6 us)
Async XLA Ops:
  66.6 7.3 copy-start
  66.6 799.9 %copy-start.7 = (s32[4]{0:T(128)S(1)}, s32[4]{0:T(128)}, u32[]{:S(2)}) copy-start(s32[4]{0:T(128)} %param.5) | copy-start | bytes 52
  66.6 860.8 %all-to-all-start = ((bf16[2,16384,512]{2,0,1:T(2,128)(2,1)}), bf16[2,16384,512]{2,0,1:T(2,128)(2,1)}, u32[]{:S(2)}, u32[]{:S(2)}) async-start(bf16[2,16384,512]{2,0,1:T(2,128)(2,1)} %copy.10), calls=%async_computation | async-start | bytes 67108864 | tf_op jit(solution)/shard_map/all_to_all | solution.py:21
  73.9 1257.3 %reduce-scatter.4.cloned.1.call-start = ((), (), s32[]{:S(2)}) async-start(), calls=%async_computation.2 | async-start | bytes 20971520
  73.9 556.5 %collective-permute-start = (bf16[2,512,512]{2,1,0:T(8,128)(2,1)S(1)}, bf16[2,512,512]{2,1,0:T(8,128)(2,1)S(1)}, u32[]{:S(2)}, u32[]{:S(2)}) collective-permute-start(bf16[2,512,512]{2,1,0:T(8,128)(2,1)S(1)} %copy-done), channel_id=1, source_target_pairs={{0,1},{1,2},{2,3},{3,4},{4,5},{5,6},{6,7},{7,0},{8,9},{9,10},{10,1... | collective-permute-start | bytes 3145736 | tf_op jit(solution)/shard_map/ppermute | solution.py:24
  630.4 16.1 %collective-permute-start.1 = (bf16[2,512,512]{2,1,0:T(8,128)(2,1)S(1)}, bf16[2,512,512]{2,1,0:T(8,128)(2,1)S(1)}, u32[]{:S(2)}, u32[]{:S(2)}) collective-permute-start(bf16[2,512,512]{2,1,0:T(8,128)(2,1)S(1)} %collective-permute-done), channel_id=1, source_target_pairs={{0,1},{1,2},{2,3},{3,4},{4,5},{5,6},{6,7},{7,0},{8,9},{9,10},{10,1... | collective-permute-start | bytes 3145736 | tf_op jit(solution)/shard_map/ppermute | solution.py:24
  646.5 16.1 %collective-permute-start.2 = (bf16[2,512,512]{2,1,0:T(8,128)(2,1)S(1)}, bf16[2,512,512]{2,1,0:T(8,128)(2,1)S(1)}, u32[]{:S(2)}, u32[]{:S(2)}) collective-permute-start(bf16[2,512,512]{2,1,0:T(8,128)(2,1)S(1)} %collective-permute-done.1), channel_id=1, source_target_pairs={{0,1},{1,2},{2,3},{3,4},{4,5},{5,6},{6,7},{7,0},{8,9},{9,10},{10,1... | collective-permute-start | bytes 3145736 | tf_op jit(solution)/shard_map/ppermute | solution.py:24
  662.6 1.0 copy-start.1
  663.6 160.6 %collective-permute-start.3 = (bf16[2,512,512]{2,1,0:T(8,128)(2,1)S(1)}, bf16[2,512,512]{2,1,0:T(8,128)(2,1)S(1)}, u32[]{:S(2)}, u32[]{:S(2)}) collective-permute-start(bf16[2,512,512]{2,1,0:T(8,128)(2,1)S(1)} %collective-permute-done.2), channel_id=1, source_target_pairs={{0,1},{1,2},{2,3},{3,4},{4,5},{5,6},{6,7},{7,0},{8,9},{9,10},{10,1... | collective-permute-start | bytes 3145736 | tf_op jit(solution)/shard_map/ppermute | solution.py:24
  824.2 1.0 copy-start.3
  825.2 16.4 %collective-permute-start.4 = (bf16[2,512,512]{2,1,0:T(8,128)(2,1)S(1)}, bf16[2,512,512]{2,1,0:T(8,128)(2,1)S(1)}, u32[]{:S(2)}, u32[]{:S(2)}) collective-permute-start(bf16[2,512,512]{2,1,0:T(8,128)(2,1)S(1)} %collective-permute-done.3), channel_id=1, source_target_pairs={{0,1},{1,2},{2,3},{3,4},{4,5},{5,6},{6,7},{7,0},{8,9},{9,10},{10,1... | collective-permute-start | bytes 3145736 | tf_op jit(solution)/shard_map/ppermute | solution.py:24
  841.6 1.0 copy-start.5
  842.6 16.2 %collective-permute-start.5 = (bf16[2,512,512]{2,1,0:T(8,128)(2,1)S(1)}, bf16[2,512,512]{2,1,0:T(8,128)(2,1)}, u32[]{:S(2)}, u32[]{:S(2)}) collective-permute-start(bf16[2,512,512]{2,1,0:T(8,128)(2,1)S(1)} %collective-permute-done.4), channel_id=1, source_target_pairs={{0,1},{1,2},{2,3},{3,4},{4,5},{5,6},{6,7},{7,0},{8,9},{9,10},{10,1... | collective-permute-start | bytes 3145736 | tf_op jit(solution)/shard_map/ppermute | solution.py:24
  858.8 16.4 %collective-permute-start.6 = (bf16[2,512,512]{2,1,0:T(8,128)(2,1)}, bf16[2,512,512]{2,1,0:T(8,128)(2,1)}, u32[]{:S(2)}, u32[]{:S(2)}) collective-permute-start(bf16[2,512,512]{2,1,0:T(8,128)(2,1)} %collective-permute-done.5), channel_id=1, source_target_pairs={{0,1},{1,2},{2,3},{3,4},{4,5},{5,6},{6,7},{7,0},{8,9},{9,10},{10,1... | collective-permute-start | bytes 3145736 | tf_op jit(solution)/shard_map/ppermute | solution.py:24
  866.5 27.8 %copy-start.6 = (bf16[2,512,512]{2,1,0:T(8,128)(2,1)S(1)}, bf16[2,512,512]{2,1,0:T(8,128)(2,1)}, u32[]{:S(2)}) copy-start(bf16[2,512,512]{2,1,0:T(8,128)(2,1)} %copy-done.5) | copy-start | bytes 3145732
  866.5 28.8 %copy-start.4 = (bf16[2,512,512]{2,1,0:T(8,128)(2,1)S(1)}, bf16[2,512,512]{2,1,0:T(8,128)(2,1)}, u32[]{:S(2)}) copy-start(bf16[2,512,512]{2,1,0:T(8,128)(2,1)} %copy-done.3) | copy-start | bytes 3145732
  866.5 29.9 %copy-start.2 = (bf16[2,512,512]{2,1,0:T(8,128)(2,1)S(1)}, bf16[2,512,512]{2,1,0:T(8,128)(2,1)}, u32[]{:S(2)}) copy-start(bf16[2,512,512]{2,1,0:T(8,128)(2,1)} %copy-done.1) | copy-start | bytes 3145732
Sparse Core Ops, SparseCore 0:
  1156.3 174.8 reduce-scatter.3
